TPU v7x, 32 devices: a whole 2x2x4 slice. The times are simulated.
32 devices in a mesh: gz: 4 (over z), gx: 4 (over y, x), gy: 2 (over core).
Axes of the slice: x: 2, y: 2, z: 4, core: 2. Of those that a mesh axis runs over, the one named last changes fastest.
Arguments:
- density: float32 [128, 256, 1024], P('gz', 'gy', 'gx'), may hold values from 0 to 1
- mask: int32 [16, 32, 128], P('gz', 'gy', 'gx'), may hold values from 0 to 3
Outputs:
- filtered: float32 [128, 256, 1024], P(('gz', 'gx'), 'gy')
- projected: float32 [128, 256, 1024], P(('gz', 'gx'), 'gy')
Inputs may be any that keep to these rules, and one draw needn't show every extreme that they name: `mask`: code 0 marks a void block, 1 a solid block, 2 and 3 design blocks.
All inputs are finite; a program needn't handle non-finite values.
Results may differ from a plain program's by a relative error of at most 0.0003.
Values sent between devices are 32-bit elements; how exact they have to be, the bound alone decides.
A program may use at most 128 MiB of HBM per device.

v0:
```python
import jax
import jax.numpy as jnp
from jax import lax
from jax.sharding import PartitionSpec as P

RADIUS = 6
CELLS = 8
sharpness = 8.0
threshold = 0.5
highest = lax.Precision.HIGHEST


def with_halo(x, sides, width):
    for axis, dim in sides:
        peers, length = (lax.axis_size(axis), x.shape[dim])
        up = [(i, (i + 1) % peers) for i in range(peers - 1)]
        down = [(j, i) for i, j in up]
        last = lax.slice_in_dim(x, length - width, length, axis=dim)
        leading = lax.slice_in_dim(x, 0, width, axis=dim)
        before = lax.ppermute(last, axis, up)
        after = lax.ppermute(leading, axis, down)
        x = jnp.concatenate([before, x, after], axis=dim)
    return x


def passed_along(block, axis, distance):
    devices = range(lax.axis_size(axis))
    route = [(i - distance, i) for i in devices if i - distance in devices]
    return lax.ppermute(block, axis, route)


def band(outputs, inputs, shift):
    out_index = lax.broadcasted_iota(jnp.int32, (outputs, inputs), 0)
    in_index = lax.broadcasted_iota(jnp.int32, (outputs, inputs), 1)
    distance = jnp.abs(in_index + shift - out_index)
    return jnp.where(distance <= RADIUS, (RADIUS + 1 - distance).astype(jnp.float32), 0.0)


def along_first(extended, count):
    kernel = band(count, count + 2 * RADIUS, -RADIUS)
    flat = extended.reshape(count + 2 * RADIUS, -1)
    result = jnp.dot(kernel, flat, precision=highest, preferred_element_type=jnp.float32)
    return result.reshape((count,) + extended.shape[1:])


def filter_last(values):
    leading = values.shape[:-1]
    extent = values.shape[-1]
    blocks = extent // 128
    widths = [(0, 0)] * (values.ndim - 1) + [(RADIUS, 128 - RADIUS)]
    padded = jnp.pad(values, widths)
    lower_part = padded[..., :extent].reshape(leading + (blocks, 128))
    upper_part = padded[..., 128 : extent + 128].reshape(leading + (blocks, 128))[..., : 2 * RADIUS]
    lower_kernel = band(128, 128, -RADIUS).T
    upper_kernel = band(128, 2 * RADIUS, 128 - RADIUS).T
    result = jnp.einsum(
        "abcd,de->abce",
        lower_part,
        lower_kernel,
        precision=highest,
        preferred_element_type=jnp.float32,
    )
    result = result + jnp.einsum(
        "abcd,de->abce",
        upper_part,
        upper_kernel,
        precision=highest,
        preferred_element_type=jnp.float32,
    )
    return result.reshape(leading + (extent,))


def one_side(reach):
    return reach * (RADIUS + 1) - reach * (reach + 1) // 2


def edge_sums(start, length, length_all):
    position = start + lax.iota(jnp.int32, length)
    reach_left = jnp.minimum(position, RADIUS)
    reach_right = jnp.minimum(length_all - 1 - position, RADIUS)
    return (RADIUS + 1 + one_side(reach_left) + one_side(reach_right)).astype(jnp.float32)


def body(density, mask):
    planes, row_count, columns = density.shape
    design_code = jnp.repeat(jnp.repeat(jnp.repeat(mask, CELLS, 0), CELLS, 1), CELLS, 2)
    physical = jnp.where(design_code == 0, 0.0, jnp.where(design_code == 1, 1.0, density))
    extended = with_halo(physical, (("gz", 0),), RADIUS)
    physical = along_first(extended, planes)
    groups = lax.axis_size("gx")
    layers = planes // groups
    gathered = lax.all_gather(physical, "gx", axis=2, tiled=True)
    own_slab = lax.dynamic_slice_in_dim(gathered, lax.axis_index("gx") * layers, layers, 0)
    smoothed = filter_last(own_slab)
    row_kernel = band(row_count + 2 * RADIUS, row_count, RADIUS)
    partial_value = jnp.einsum(
        "wy,zyx->zwx", row_kernel, smoothed, precision=highest, preferred_element_type=jnp.float32
    )
    from_previous = passed_along(partial_value[:, row_count + RADIUS :], "gy", 1)
    from_next = passed_along(partial_value[:, :RADIUS], "gy", -1)
    summed = partial_value[:, RADIUS : row_count + RADIUS]
    summed = summed.at[:, :RADIUS].add(from_previous)
    summed = summed.at[:, row_count - RADIUS :].add(from_next)
    width_all = summed.shape[2]
    count_x = edge_sums(0, width_all, width_all)
    count_y = edge_sums(
        lax.axis_index("gy") * row_count, row_count, row_count * lax.axis_size("gy")
    )
    count_z = edge_sums(lax.axis_index(("gz", "gx")) * layers, layers, planes * lax.axis_size("gz"))
    counts = count_z[:, None, None] * count_y[None, :, None] * count_x[None, None, :]
    filtered = summed / counts
    top = jnp.tanh(sharpness * threshold)
    projected = (top + jnp.tanh(sharpness * (filtered - threshold))) / (
        top + jnp.tanh(sharpness * (1.0 - threshold))
    )
    return (filtered, projected)


def solution(mesh):
    placed = (P("gz", "gy", "gx"), P("gz", "gy", "gx"))
    return jax.shard_map(
        body,
        mesh=mesh,
        in_specs=placed,
        out_specs=(P(("gz", "gx"), "gy", None), P(("gz", "gx"), "gy", None)),
        check_vma=False,
    )
```

profile of v0, /device:TPU:1, one launch (start us, length us, event | category | flops | bytes accessed | tf_op | source)
XLA Modules:
  0.0 268.6 jit_solution(17952805797014648781)
XLA Ops:
  7.2 0.0 all-gather.2.cloned.1.call-start
  7.2 5.6 %copy.16 = f32[32,128,256]{1,2,0:T(8,128)} copy(f32[32,128,256]{2,1,0:T(8,128)} %param.6) | data formatting | bytes 8388608 | tf_op args[0]
  12.8 0.3 broadcast_bitcast_fusion
  13.1 0.6 copy.15
  13.8 0.3 broadcast_bitcast_fusion.1
  14.1 0.6 copy.14
  14.8 3.3 %select_select_fusion = f32[32,128,256]{1,2,0:T(8,128)S(1)} fusion(f32[32,128,256]{1,2,0:T(8,128)} %copy.16, pred[32,128,32]{1,2,0:T(8,128)(4,1)S(1)} %copy.15, pred[32,128,32]{1,2,0:T(8,128)(4,1)S(1)} %copy.14), kind=kLoop, calls=%fused_computation.14 | loop fusion | flops 2097152 | bytes 8650752 | tf_op jit(solution)/shard_map/jit(_where)/select_n | solution.py:87
  18.0 0.1 fusion.86
  18.2 1.3 collective-permute-start.1
  19.5 4.7 %collective-permute-start = (f32[6,128,256]{1,2,0:T(8,128)S(1)}, f32[6,128,256]{1,2,0:T(8,128)S(1)}, u32[]{:S(2)}, u32[]{:S(2)}) collective-permute-start(f32[6,128,256]{1,2,0:T(8,128)S(1)} %get-tuple-element.32), channel_id=1, source_target_pairs={{0,8},{8,16},{16,24},{1,9},{9,17},{17,25},{2,10},{10,18},{18,26},{... | collective-permute-start | bytes 2359304 | tf_op jit(solution)/shard_map/ppermute | solution.py:20
  24.2 15.2 %collective-permute-done.1 = f32[6,128,256]{1,2,0:T(8,128)S(1)} collective-permute-done((f32[6,128,256]{1,2,0:T(8,128)S(1)}, f32[6,128,256]{1,2,0:T(8,128)S(1)}, u32[]{:S(2)}, u32[]{:S(2)}) %collective-permute-start.1) | collective-permute-done | bytes 786464 | tf_op jit(solution)/shard_map/ppermute | solution.py:21
  39.4 0.9 collective-permute-done
  40.3 2.9 %pad_maximum_fusion = f32[44,128,256]{1,2,0:T(8,128)} fusion(f32[6,128,256]{1,2,0:T(8,128)S(1)} %collective-permute-done.1, f32[32,128,256]{1,2,0:T(8,128)S(1)} %select_select_fusion, f32[6,128,256]{1,2,0:T(8,128)S(1)} %collective-permute-done), kind=kLoop, calls=%fused_computation.3 | loop fusion | flops 2883584 | bytes 11534336 | tf_op jit(solution)/shard_map/concatenate | solution.py:22
  43.2 6.3 %copy.17 = f32[44,128,256]{2,1,0:T(8,128)} copy(f32[44,128,256]{1,2,0:T(8,128)} %pad_maximum_fusion) | data formatting | bytes 11534336 | tf_op jit(solution)/shard_map/concatenate | solution.py:22
  49.4 3.3 %slice_bitcast_fusion = f32[128,256,44]{1,0,2:T(8,128)S(1)} fusion(f32[44,128,256]{2,1,0:T(8,128)} %copy.17), kind=kLoop, calls=%fused_computation.2 | loop fusion | bytes 11534336 | tf_op jit(solution)/shard_map/dot_general | solution.py:42
  52.7 8.2 %fusion = f32[32,128,256]{2,0,1:T(8,128)} fusion(f32[128,256,44]{1,0,2:T(8,128)S(1)} %slice_bitcast_fusion, s32[44]{0:T(128)S(1)} %iota_add_fusion.3), kind=kOutput, calls=%fused_computation | convolution fusion | flops 553656576 | bytes 9961648 | tf_op jit(solution)/shard_map/dot_general | solution.py:42
  60.9 0.0 all-gather.2.cloned.1.call-update
  61.0 160.3 %all-gather.2.cloned.1.call-done = f32[32,128,1024]{2,0,1:T(8,128)} async-done(((f32[32,128,256]{2,0,1:T(8,128)}), f32[32,128,1024]{2,0,1:T(8,128)}) %all-gather.2.cloned.1.call-update) | async-done | bytes 16777232 | tf_op jit(solution)/shard_map/all_gather | solution.py:92
  221.3 2.5 constant_dynamic-slice_fusion
  223.8 2.2 fusion.2
  226.0 6.4 %fusion.4 = f32[8,128,8,128]{1,3,2,0:T(8,128)S(1)} fusion(f32[8,128,8,12]{3,0,2,1:T(8,128)S(1)} %bitcast.47, s32[12]{0:T(128)S(1)} %iota_add_fusion.1), kind=kOutput, calls=%fused_computation.8 | convolution fusion | flops 151004160 | bytes 4587568 | tf_op jit(solution)/shard_map/abcd,de->abce/dot_general | solution.py:63
  232.5 6.5 %fusion.8 = f32[8,128,8,128]{1,3,2,0:T(8,128)S(1)} fusion(f32[8,128,8,128]{1,3,2,0:T(8,128)S(1)} %fusion.4, f32[8,128,8,128]{3,0,2,1:T(8,128)S(1)} %get-tuple-element.30, s32[128]{0:T(128)S(1)} %iota_add_fusion.2), kind=kOutput, calls=%fused_computation.16 | convolution fusion | flops 1611759616 | bytes 12583424 | tf_op jit(solution)/shard_map/abcd,de->abce/dot_general | solution.py:56
  239.0 4.4 %convolution_bitcast_fusion = f32[8,140,1024]{2,1,0:T(8,128)S(1)} fusion(f32[8,128,1024]{1,2,0:T(8,128)S(1)} %bitcast.48, s32[128]{0:T(128)S(1)} %iota_add_fusion), kind=kOutput, calls=%fused_computation.15 | convolution fusion | flops 1761715200 | bytes 8782336 | tf_op jit(solution)/shard_map/wy,zyx->zwx/dot_general | solution.py:96
  243.4 0.1 fusion.85
  243.4 1.3 collective-permute-start.2
  244.7 0.1 broadcast_multiply_fusion
  244.8 2.5 slice.86
  247.3 3.1 %collective-permute-start.3 = (f32[8,6,1024]{2,1,0:T(8,128)S(1)}, f32[8,6,1024]{2,1,0:T(8,128)S(1)}, u32[]{:S(2)}, u32[]{:S(2)}) collective-permute-start(f32[8,6,1024]{2,1,0:T(8,128)S(1)} %get-tuple-element.28), channel_id=1, source_target_pairs={{1,0},{3,2},{5,4},{7,6},{9,8},{11,10},{13,12},{15,14},{17,16},{19,... | collective-permute-start | bytes 589832 | tf_op jit(solution)/shard_map/ppermute | solution.py:29
  250.5 1.8 scatter-add.6
  252.3 1.0 slice_add_fusion
  253.3 1.7 scatter-add.9
  255.0 6.8 %add_multiply_fusion = (f32[8,128,1024]{2,1,0:T(8,128)}, f32[8,128,1024]{2,1,0:T(8,128)}) fusion(f32[8,128,1024]{2,1,0:T(8,128)} %scatter-add.9, f32[1024]{0:T(1024)S(1)} %fusion.56, f32[8,128]{1,0:T(8,128)S(1)} %broadcast_multiply_fusion), kind=kLoop, calls=%fused_computation.12 | loop fusion | flops 6291456 | bytes 12591104 | tf_op jit(solution)/shard_map/div | solution.py:113
  (15 shorter events, 0.2 us)
Async XLA Ops:
  7.2 5.6 %copy-start = (s32[4,16,32]{2,1,0:T(8,128)S(1)}, s32[4,16,32]{2,1,0:T(8,128)}, u32[]{:S(2)}) copy-start(s32[4,16,32]{2,1,0:T(8,128)} %param.7) | copy-start | bytes 24580
  7.2 214.1 %all-gather.2.cloned.1.call-start = ((), (), s32[]{:S(2)}) async-start(), calls=%async_computation | async-start | bytes 20971520 | tf_op jit(solution)/shard_map/all_gather | solution.py:92
  18.2 21.3 %collective-permute-start.1 = (f32[6,128,256]{1,2,0:T(8,128)S(1)}, f32[6,128,256]{1,2,0:T(8,128)S(1)}, u32[]{:S(2)}, u32[]{:S(2)}) collective-permute-start(f32[6,128,256]{1,2,0:T(8,128)S(1)} %get-tuple-element.33), channel_id=1, source_target_pairs={{8,0},{16,8},{24,16},{9,1},{17,9},{25,17},{10,2},{18,10},{26,18},{... | collective-permute-start | bytes 2359304 | tf_op jit(solution)/shard_map/ppermute | solution.py:21
  19.5 20.9 %collective-permute-start = (f32[6,128,256]{1,2,0:T(8,128)S(1)}, f32[6,128,256]{1,2,0:T(8,128)S(1)}, u32[]{:S(2)}, u32[]{:S(2)}) collective-permute-start(f32[6,128,256]{1,2,0:T(8,128)S(1)} %get-tuple-element.32), channel_id=1, source_target_pairs={{0,8},{8,16},{16,24},{1,9},{9,17},{17,25},{2,10},{10,18},{18,26},{... | collective-permute-start | bytes 2359304 | tf_op jit(solution)/shard_map/ppermute | solution.py:20
  243.4 7.0 %collective-permute-start.2 = (f32[8,6,1024]{2,1,0:T(8,128)S(1)}, f32[8,6,1024]{2,1,0:T(8,128)S(1)}, u32[]{:S(2)}, u32[]{:S(2)}) collective-permute-start(f32[8,6,1024]{2,1,0:T(8,128)S(1)} %get-tuple-element.29), channel_id=1, source_target_pairs={{0,1},{2,3},{4,5},{6,7},{8,9},{10,11},{12,13},{14,15},{16,17},{18,... | collective-permute-start | bytes 589832 | tf_op jit(solution)/shard_map/ppermute | solution.py:29
  247.3 4.9 %collective-permute-start.3 = (f32[8,6,1024]{2,1,0:T(8,128)S(1)}, f32[8,6,1024]{2,1,0:T(8,128)S(1)}, u32[]{:S(2)}, u32[]{:S(2)}) collective-permute-start(f32[8,6,1024]{2,1,0:T(8,128)S(1)} %get-tuple-element.28), channel_id=1, source_target_pairs={{1,0},{3,2},{5,4},{7,6},{9,8},{11,10},{13,12},{15,14},{17,16},{19,... | collective-permute-start | bytes 589832 | tf_op jit(solution)/shard_map/ppermute | solution.py:29
Sparse Core Ops, SparseCore 0:
  61.1 160.2 all-gather.1
where the time goes:
time: 269 us
  waiting for transfers between devices  176 us (65%)
  local copies, waits for them, and re-layouts  28 us (10%)
  matrix products  25.5 us (9%)
  between operations  14.2 us (5%)
  other arithmetic  14.1 us (5%)
  starting transfers between devices  10.4 us (4%)
    all_gather x1, waiting for transfers between devices, body(): gathered = lax.all_gather(physical, 'gx', axis=2, tiled=True)  160 us
    ppermute x1, waiting for transfers between devices, with_halo(): after = lax.ppermute(leading, axis, down)  15.2 us
    dot_general x1, matrix products, along_first(): jnp.dot(kernel, flat, precision=highest, preferred_element_type=jnp.float32)  8.16 us
    div x1, other arithmetic, body(): (top + jnp.tanh(sharpness * (filtered - threshold))) / (top + jnp.tanh(sh...  6.76 us
    dot_general x1, matrix products, filter_last(): jnp.einsum('abcd,de->abce', lower_part, lower_kernel, precision=highest,...  6.49 us
    dot_general x1, matrix products, filter_last(): jnp.einsum('abcd,de->abce', upper_part, upper_kernel, precision=highest,...  6.43 us
    concatenate x1, local copies, waits for them, and re-layouts, with_halo(): x = jnp.concatenate([before, x, after], axis=dim)  6.27 us
    unnamed x3, local copies, waits for them, and re-layouts  5.58 us
  transfers between devices with their start and end apart: 5, of which 3 were waited for; matrix products, arithmetic and copies ran while one was open for 2% of the time, Pallas kernels for 0%

commit v1 on v0

--- a/solution.py
+++ b/solution.py
@@ -89,7 +89,7 @@
     physical = along_first(extended, planes)
     groups = lax.axis_size("gx")
     layers = planes // groups
-    gathered = lax.all_gather(physical, "gx", axis=2, tiled=True)
+    gathered = jnp.concatenate(lax.all_gather(physical, "gx"), axis=2)
     own_slab = lax.dynamic_slice_in_dim(gathered, lax.axis_index("gx") * layers, layers, 0)
     smoothed = filter_last(own_slab)
     row_kernel = band(row_count + 2 * RADIUS, row_count, RADIUS)

time: 269 us -> 282 us (1.048)
  local copies, waits for them, and re-layouts: 28 us -> 45.9 us
  matrix products: 25.5 us -> 20.2 us
    all_gather x0 -> x1, local copies, waits for them, and re-layouts: none -> 19.4 us  [body(): gathered = jnp.concatenate(lax.all_gather(physical, 'gx'), axis=2)]
    dot_general x1, matrix products: 6.43 us -> 3.53 us  [filter_last(): jnp.einsum('abcd,de->abce', upper_part, upper_kernel, precision=highest,...]
where the time goes in v1:
time: 282 us; the launch traced here: 281 us
  waiting for transfers between devices  177 us (63%)
  local copies, waits for them, and re-layouts  45.9 us (16%)
  matrix products  20.2 us (7%)
  between operations  14.3 us (5%)
  other arithmetic  14.1 us (5%)
  starting transfers between devices  10.4 us (4%)
    all_gather x1, waiting for transfers between devices, body(): gathered = jnp.concatenate(lax.all_gather(physical, 'gx'), axis=2)  160 us
    all_gather x1, local copies, waits for them, and re-layouts, body(): gathered = jnp.concatenate(lax.all_gather(physical, 'gx'), axis=2)  19.4 us
    ppermute x1, waiting for transfers between devices, with_halo(): after = lax.ppermute(leading, axis, down)  15.2 us
    dot_general x1, matrix products, along_first(): jnp.dot(kernel, flat, precision=highest, preferred_element_type=jnp.float32)  8.16 us
    div x1, other arithmetic, body(): (top + jnp.tanh(sharpness * (filtered - threshold))) / (top + jnp.tanh(sh...  6.76 us
    concatenate x1, local copies, waits for them, and re-layouts, with_halo(): x = jnp.concatenate([before, x, after], axis=dim)  6.27 us
  transfers between devices with their start and end apart: 5, of which 3 were waited for; matrix products, arithmetic and copies ran while one was open for 2% of the time, Pallas kernels for 0%

profile of v1, /device:TPU:1, one launch (start us, length us, event | category | flops | bytes accessed | tf_op | source)
XLA Modules:
  0.0 281.4 jit_solution(2288144835151656896)
XLA Ops:
  7.2 0.0 all-gather.3.cloned.1.call-start
  7.2 5.6 %copy.14 = f32[32,128,256]{1,2,0:T(8,128)} copy(f32[32,128,256]{2,1,0:T(8,128)} %param.6) | data formatting | bytes 8388608 | tf_op args[0]
  12.8 0.3 broadcast_bitcast_fusion
  13.1 0.6 copy.13
  13.8 0.3 broadcast_bitcast_fusion.1
  14.1 0.6 copy.12
  14.8 3.3 %select_select_fusion = f32[32,128,256]{1,2,0:T(8,128)S(1)} fusion(f32[32,128,256]{1,2,0:T(8,128)} %copy.14, pred[32,128,32]{1,2,0:T(8,128)(4,1)S(1)} %copy.13, pred[32,128,32]{1,2,0:T(8,128)(4,1)S(1)} %copy.12), kind=kLoop, calls=%fused_computation.8 | loop fusion | flops 2097152 | bytes 8650752 | tf_op jit(solution)/shard_map/jit(_where)/select_n | solution.py:87
  18.0 0.1 fusion.79
  18.2 1.3 collective-permute-start.1
  19.5 4.7 %collective-permute-start = (f32[6,128,256]{1,2,0:T(8,128)S(1)}, f32[6,128,256]{1,2,0:T(8,128)S(1)}, u32[]{:S(2)}, u32[]{:S(2)}) collective-permute-start(f32[6,128,256]{1,2,0:T(8,128)S(1)} %get-tuple-element.32), channel_id=1, source_target_pairs={{0,8},{8,16},{16,24},{1,9},{9,17},{17,25},{2,10},{10,18},{18,26},{... | collective-permute-start | bytes 2359304 | tf_op jit(solution)/shard_map/ppermute | solution.py:20
  24.2 15.2 %collective-permute-done.1 = f32[6,128,256]{1,2,0:T(8,128)S(1)} collective-permute-done((f32[6,128,256]{1,2,0:T(8,128)S(1)}, f32[6,128,256]{1,2,0:T(8,128)S(1)}, u32[]{:S(2)}, u32[]{:S(2)}) %collective-permute-start.1) | collective-permute-done | bytes 786464 | tf_op jit(solution)/shard_map/ppermute | solution.py:21
  39.4 0.9 collective-permute-done
  40.3 2.9 %pad_maximum_fusion = f32[44,128,256]{1,2,0:T(8,128)} fusion(f32[6,128,256]{1,2,0:T(8,128)S(1)} %collective-permute-done.1, f32[32,128,256]{1,2,0:T(8,128)S(1)} %select_select_fusion, f32[6,128,256]{1,2,0:T(8,128)S(1)} %collective-permute-done), kind=kLoop, calls=%fused_computation.3 | loop fusion | flops 2883584 | bytes 11534336 | tf_op jit(solution)/shard_map/concatenate | solution.py:22
  43.2 6.3 %copy.15 = f32[44,128,256]{2,1,0:T(8,128)} copy(f32[44,128,256]{1,2,0:T(8,128)} %pad_maximum_fusion) | data formatting | bytes 11534336 | tf_op jit(solution)/shard_map/concatenate | solution.py:22
  49.4 3.3 %slice_bitcast_fusion = f32[128,256,44]{1,0,2:T(8,128)S(1)} fusion(f32[44,128,256]{2,1,0:T(8,128)} %copy.15), kind=kLoop, calls=%fused_computation.2 | loop fusion | bytes 11534336 | tf_op jit(solution)/shard_map/dot_general | solution.py:42
  52.7 8.2 %fusion = f32[32,128,256]{2,0,1:T(8,128)} fusion(f32[128,256,44]{1,0,2:T(8,128)S(1)} %slice_bitcast_fusion, s32[44]{0:T(128)S(1)} %iota_add_fusion.3), kind=kOutput, calls=%fused_computation | convolution fusion | flops 553656576 | bytes 9961648 | tf_op jit(solution)/shard_map/dot_general | solution.py:42
  61.0 160.4 %all-gather.3.cloned.1.call-done = f32[128,128,256]{2,0,1:T(8,128)} async-done(((f32[32,128,256]{2,0,1:T(8,128)}), f32[128,128,256]{2,0,1:T(8,128)}) %all-gather.3.cloned.1.call-update) | async-done | bytes 16777232 | tf_op jit(solution)/shard_map/all_gather | solution.py:92
  221.4 19.4 %copy.17 = f32[4,32,128,256]{2,3,0,1:T(8,128)} copy(f32[4,32,128,256]{3,1,0,2:T(8,128)} %bitcast.51) | data formatting | bytes 33554432 | tf_op jit(solution)/shard_map/all_gather | solution.py:92
  240.9 2.5 constant_dynamic-slice_fusion
  243.4 0.7 pad_slice_fusion.1
  244.1 3.5 %fusion.2 = f32[8,128,8,128]{1,3,2,0:T(8,128)S(1)} fusion(f32[8,128,8,128]{1,3,2,0:T(8,128)S(1)} %bitcast.53, s32[12]{0:T(128)S(1)} %iota_add_fusion.1), kind=kOutput, calls=%fused_computation.13 | convolution fusion | flops 151004160 | bytes 4719104 | tf_op jit(solution)/shard_map/abcd,de->abce/dot_general | solution.py:63
  247.6 3.9 %convolution_add_fusion = f32[8,128,8,128]{1,3,2,0:T(8,128)S(1)} fusion(f32[8,128,8,128]{1,3,2,0:T(8,128)S(1)} %fusion.2, f32[8,128,8,128]{1,3,2,0:T(8,128)S(1)} %bitcast.50, s32[128]{0:T(128)S(1)} %iota_add_fusion.2), kind=kOutput, calls=%fused_computation.10 | convolution fusion | flops 1611759616 | bytes 12583424 | tf_op jit(solution)/shard_map/abcd,de->abce/dot_general | solution.py:56
  251.5 4.6 %convolution_bitcast_fusion = f32[8,140,1024]{2,1,0:T(8,128)S(1)} fusion(f32[8,128,1024]{1,2,0:T(8,128)S(1)} %bitcast.52, s32[128]{0:T(128)S(1)} %iota_add_fusion), kind=kOutput, calls=%fused_computation.9 | convolution fusion | flops 1761715200 | bytes 8782336 | tf_op jit(solution)/shard_map/wy,zyx->zwx/dot_general | solution.py:96
  256.2 0.1 fusion.78
  256.2 1.3 collective-permute-start.2
  257.5 0.1 broadcast_multiply_fusion
  257.6 2.5 slice.86
  260.1 3.1 %collective-permute-start.3 = (f32[8,6,1024]{2,1,0:T(8,128)S(1)}, f32[8,6,1024]{2,1,0:T(8,128)S(1)}, u32[]{:S(2)}, u32[]{:S(2)}) collective-permute-start(f32[8,6,1024]{2,1,0:T(8,128)S(1)} %get-tuple-element.28), channel_id=1, source_target_pairs={{1,0},{3,2},{5,4},{7,6},{9,8},{11,10},{13,12},{15,14},{17,16},{19,... | collective-permute-start | bytes 589832 | tf_op jit(solution)/shard_map/ppermute | solution.py:29
  263.3 1.8 scatter-add.6
  265.1 1.0 slice_add_fusion
  266.1 1.7 scatter-add.9
  267.8 6.8 %add_multiply_fusion = (f32[8,128,1024]{2,1,0:T(8,128)}, f32[8,128,1024]{2,1,0:T(8,128)}) fusion(f32[8,128,1024]{2,1,0:T(8,128)} %scatter-add.9, f32[1024]{0:T(1024)S(1)} %fusion.49, f32[8,128]{1,0:T(8,128)S(1)} %broadcast_multiply_fusion), kind=kLoop, calls=%fused_computation.6 | loop fusion | flops 6291456 | bytes 12591104 | tf_op jit(solution)/shard_map/div | solution.py:113
  (16 shorter events, 0.2 us)
Async XLA Ops:
  7.2 5.6 %copy-start = (s32[4,16,32]{2,1,0:T(8,128)S(1)}, s32[4,16,32]{2,1,0:T(8,128)}, u32[]{:S(2)}) copy-start(s32[4,16,32]{2,1,0:T(8,128)} %param.7) | copy-start | bytes 24580
  7.2 214.3 %all-gather.3.cloned.1.call-start = ((), (), s32[]{:S(2)}) async-start(), calls=%async_computation | async-start | bytes 20971520 | tf_op jit(solution)/shard_map/all_gather | solution.py:92
  18.2 21.3 %collective-permute-start.1 = (f32[6,128,256]{1,2,0:T(8,128)S(1)}, f32[6,128,256]{1,2,0:T(8,128)S(1)}, u32[]{:S(2)}, u32[]{:S(2)}) collective-permute-start(f32[6,128,256]{1,2,0:T(8,128)S(1)} %get-tuple-element.33), channel_id=1, source_target_pairs={{8,0},{16,8},{24,16},{9,1},{17,9},{25,17},{10,2},{18,10},{26,18},{... | collective-permute-start | bytes 2359304 | tf_op jit(solution)/shard_map/ppermute | solution.py:21
  19.5 20.9 %collective-permute-start = (f32[6,128,256]{1,2,0:T(8,128)S(1)}, f32[6,128,256]{1,2,0:T(8,128)S(1)}, u32[]{:S(2)}, u32[]{:S(2)}) collective-permute-start(f32[6,128,256]{1,2,0:T(8,128)S(1)} %get-tuple-element.32), channel_id=1, source_target_pairs={{0,8},{8,16},{16,24},{1,9},{9,17},{17,25},{2,10},{10,18},{18,26},{... | collective-permute-start | bytes 2359304 | tf_op jit(solution)/shard_map/ppermute | solution.py:20
  256.2 7.0 %collective-permute-start.2 = (f32[8,6,1024]{2,1,0:T(8,128)S(1)}, f32[8,6,1024]{2,1,0:T(8,128)S(1)}, u32[]{:S(2)}, u32[]{:S(2)}) collective-permute-start(f32[8,6,1024]{2,1,0:T(8,128)S(1)} %get-tuple-element.29), channel_id=1, source_target_pairs={{0,1},{2,3},{4,5},{6,7},{8,9},{10,11},{12,13},{14,15},{16,17},{18,... | collective-permute-start | bytes 589832 | tf_op jit(solution)/shard_map/ppermute | solution.py:29
  260.1 4.9 %collective-permute-start.3 = (f32[8,6,1024]{2,1,0:T(8,128)S(1)}, f32[8,6,1024]{2,1,0:T(8,128)S(1)}, u32[]{:S(2)}, u32[]{:S(2)}) collective-permute-start(f32[8,6,1024]{2,1,0:T(8,128)S(1)} %get-tuple-element.28), channel_id=1, source_target_pairs={{1,0},{3,2},{5,4},{7,6},{9,8},{11,10},{13,12},{15,14},{17,16},{19,... | collective-permute-start | bytes 589832 | tf_op jit(solution)/shard_map/ppermute | solution.py:29
Sparse Core Ops, SparseCore 0:
  61.1 160.3 all-gather.2
